TPU v7x, 8 devices: a whole 2x2x1 slice. The times are simulated.
8 devices in a mesh: dp: 1 (over z), col: 2 (over y), row: 4 (over x, core).
Axes of the slice: x: 2, y: 2, z: 1, core: 2. Of those that a mesh axis runs over, the one named last changes fastest.
Arguments:
- latent: bfloat16 [16, 16, 96, 384], P('dp', 'row', 'col')
- t_emb: bfloat16 [16, 768], P('dp')
- res_norm: bfloat16 [2, 2, 2, 384], replicated
- res_conv: bfloat16 [2, 2, 3, 3, 384, 384], replicated
- res_temb: bfloat16 [2, 768, 384], replicated
- attn_norm: bfloat16 [2, 384], replicated
- attn_proj: bfloat16 [4, 12, 384, 32], replicated
Outputs:
- output: bfloat16 [16, 16, 96, 384], P('dp', 'row', 'col')
All inputs are finite; a program needn't handle non-finite values.
Results may differ from a plain program's by a relative error of at most 0.00941283.
Values are sent between devices in bfloat16 or wider.
A program may use at most 1 GiB of HBM per device.

v0:
```python
import functools

import jax
import jax.numpy as jnp
from jax import lax
from jax.experimental import pallas as pl
from jax.experimental.pallas import tpu as pltpu
from jax.sharding import PartitionSpec as P

MESH = pl.DeviceIdType.MESH
GROUPS = 32
EPS = 1e-5
LOG2E = 1.4426950408889634
F32 = jnp.float32
BF16 = jnp.bfloat16
Q_TILE = 512
K_CHUNK = 256
AHEAD = 2
CHUNK = 768
LAST_CHUNK = 512
PROJ_TILE = 512


def _me_and_peers(n_row, n_col):
    me_r, me_c = lax.axis_index('row'), lax.axis_index('col')
    peers = []
    for k in range(1, n_row * n_col):
        peers.append((lax.rem(me_r + k // n_col, n_row), lax.rem(me_c + k % n_col, n_col)))
    return me_r, me_c, peers


def _barrier(peers):
    sem = pltpu.get_barrier_semaphore()
    for r, c in peers:
        pl.semaphore_signal(sem, inc=1, device_id={'row': r, 'col': c}, device_id_type=MESH)
    pl.semaphore_wait(sem, len(peers))


def _dot(a, b, dims=((1,), (0,))):
    return lax.dot_general(a, b, (dims, ((), ())), preferred_element_type=F32)


def _chan_sums(v):
    return jnp.sum(v, axis=0, keepdims=True), jnp.sum(v * v, axis=0, keepdims=True)


def _group_matrix(n_ch):
    per = n_ch // GROUPS
    gi = lax.broadcasted_iota(jnp.int32, (n_ch, n_ch), 0) // per
    gj = lax.broadcasted_iota(jnp.int32, (n_ch, n_ch), 1) // per
    return jnp.where(gi == gj, 1.0, 0.0).astype(BF16)


def _moments(s1, s2, grp, count):
    n_ch = s1.shape[1]
    st = jnp.concatenate([s1, s2, jnp.zeros((6, n_ch), F32)], axis=0)
    hi = st.astype(BF16)
    r1 = st - hi.astype(F32)
    mid = r1.astype(BF16)
    lo = (r1 - mid.astype(F32)).astype(BF16)
    tot = (_dot(lo, grp) + _dot(mid, grp)) + _dot(hi, grp)
    mean = tot[0:1] / count
    var = tot[1:2] / count - mean * mean
    return mean, lax.rsqrt(var + EPS)


def _zero_sums(n_ch):
    return jnp.zeros((1, n_ch), F32), jnp.zeros((1, n_ch), F32)


class _ResBlock:
    def __init__(self, hh, ww, n_ch, rnorm_ref, w_t, act, hid, temb_s, grp_s, sums_s):
        self.hh, self.ww, self.n_ch = hh, ww, n_ch
        self.rnorm_ref, self.w_t, self.act, self.hid = rnorm_ref, w_t, act, hid
        self.temb_s, self.grp_s, self.sums_s = temb_s, grp_s, sums_s
        self.count = float(hh * ww * (n_ch // GROUPS))

    def setup(self, temb_ref, wtemb_ref):
        te = temb_ref[...].astype(F32)
        t_act = (te * jax.nn.sigmoid(te)).astype(BF16)
        self.temb_s[...] = _dot(t_act, wtemb_ref[...])
        self.grp_s[...] = _group_matrix(self.n_ch)
        zeros = jnp.zeros((self.ww, self.act.shape[1]), BF16)
        self.act[0:self.ww, :] = zeros
        self.act[(self.hh + 1) * self.ww:(self.hh + 2) * self.ww, :] = zeros

    def conv(self, j, src, sums, chunk, epilogue):
        ww, n_ch, act = self.ww, self.n_ch, self.act
        mean, inv = _moments(*sums, self.grp_s[...], self.count)
        a_mul = inv * self.rnorm_ref[j, 0:1].astype(F32)
        b_add = self.rnorm_ref[j, 1:2].astype(F32)
        col = lax.broadcasted_iota(jnp.int32, (ww, 1), 0)

        def fill(i):
            u = (src(i * ww, ww).astype(F32) - mean) * a_mul + b_add
            a = u * (0.5 * jnp.tanh(0.5 * u) + 0.5)
            left = jnp.where(col == 0, 0.0, pltpu.roll(a, 1, 0))
            right = jnp.where(col == ww - 1, 0.0, pltpu.roll(a, ww - 1, 0))
            d0 = (i + 1) * ww
            act[d0:d0 + ww, 0:n_ch] = left.astype(BF16)
            act[d0:d0 + ww, n_ch:2 * n_ch] = a.astype(BF16)
            act[d0:d0 + ww, 2 * n_ch:3 * n_ch] = right.astype(BF16)

        def need(n):
            return min(self.hh, -(-(n + ww) // ww))

        n_pos = self.hh * ww
        for i in range(need(chunk)):
            fill(i)
        s1, s2 = _zero_sums(n_ch)
        for r0 in range(0, n_pos, chunk):
            lhs = jnp.concatenate([act[r0 + dy * ww:r0 + dy * ww + chunk, :] for dy in range(3)], axis=1)
            acc = _dot(self.w_t[j], lhs, ((1,), (1,)))
            for i in range(need(r0 + chunk), need(min(n_pos, r0 + 2 * chunk))):
                fill(i)
            out = epilogue(r0, acc.T)
            d1, d2 = _chan_sums(out.astype(F32))
            s1, s2 = s1 + d1, s2 + d2
        self.sums_s[0:1] = s1
        self.sums_s[1:2] = s2

    def run(self, src, sums, img, last_chunk, dst):
        hid, sums_s = self.hid, self.sums_s
        t_row = self.temb_s[pl.ds(img, 1), :]

        def first(r0, acc):
            out = (acc + t_row).astype(BF16)
            hid[r0:r0 + out.shape[0]] = out
            return out

        def second(r0, acc):
            out = (src(r0, acc.shape[0]).astype(F32) + acc).astype(BF16)
            dst(r0, out)
            return out

        self.conv(0, src, sums, CHUNK, first)

        @pl.when(img >= 0)
        def _():
            self.conv(1, lambda r0, n: hid[r0:r0 + n], (sums_s[0:1], sums_s[1:2]), last_chunk, second)


def _first_kernel(n_row, n_col, lat_ref, temb_hbm, rnorm_hbm, conv_hbm, wtemb_hbm, o_ref, sums_ref, next_w,
                  xv, wconv, w_t, temb_v, rnorm_v, wtemb, act, hid, temb_s, grp_s, sums_s, wsem, send_sem, recv_sem, loc_sem):
    me_r, me_c, peers = _me_and_peers(n_row, n_col)
    me = me_r * n_col + me_c
    n_img, hh, ww, n_ch = xv.shape
    bh, bw = hh // n_row, ww // n_col
    weights = [pltpu.make_async_copy(conv_hbm.at[i // 2, i % 2], wconv.at[i], wsem.at[i]) for i in range(4)]
    small = [
        pltpu.make_async_copy(wtemb_hbm.at[0], wtemb, wsem.at[4]),
        pltpu.make_async_copy(temb_hbm, temb_v, wsem.at[5]),
        pltpu.make_async_copy(rnorm_hbm, rnorm_v, wsem.at[6]),
    ]

    def place(s):
        return xv.at[s, pl.ds(me_r * bh, bh), pl.ds(pl.multiple_of(me_c * bw, bw), bw), :]

    def copy(s, k):
        r, c = peers[k]
        return pltpu.make_async_remote_copy(
            lat_ref.at[(r * n_col + c) * n_img + s], place(s), send_sem.at[s, k], recv_sem.at[s, k],
            device_id={'row': r, 'col': c}, device_id_type=MESH)

    def own(s):
        return pltpu.make_async_copy(lat_ref.at[me * n_img + s], place(s), loc_sem.at[s])

    _barrier(peers)
    for s in range(n_img):
        for k in range(len(peers)):
            copy(s, k).start()
        own(s).start()
    for w in [*small, *weights]:
        w.start()

    blk = _ResBlock(hh, ww, n_ch, rnorm_v.at[0], w_t, act, hid, temb_s, grp_s, sums_s)
    for w in small:
        w.wait()
    blk.setup(temb_v, wtemb)
    for w in weights:
        w.wait()

    def turn(i, carry):
        t0 = pl.multiple_of(i * n_ch, n_ch)
        for j in range(4):
            out = w_t.at[j] if j < 2 else next_w.at[j - 2]
            out[:, pl.ds(t0, n_ch)] = wconv[j, pl.ds(t0, n_ch), :].T
        return carry

    lax.fori_loop(0, 9, turn, 0)

    def image(s, carry):
        for k in range(len(peers)):
            copy(s, k).wait_recv()
        own(s).wait()

        def src(r0, n):
            return xv[s, pl.ds(r0 // ww, n // ww)].reshape(n, n_ch)

        def in_sums(i, sums):
            d1, d2 = _chan_sums(src(i * 4 * ww, 4 * ww).astype(F32))
            return sums[0] + d1, sums[1] + d2

        def dst(r0, v):
            o_ref[s, r0:r0 + v.shape[0]] = v

        sums = lax.fori_loop(0, hh // 4, in_sums, _zero_sums(n_ch))
        blk.run(src, sums, me * n_img + s, CHUNK, dst)
        sums_ref[s] = sums_s[...]
        return carry

    lax.fori_loop(0, n_img, image, 0)
    for s in range(n_img):
        for k in range(len(peers)):
            copy(s, k).wait_send()


def _last_kernel(n_row, n_col, x_ref, sums_ref, temb_ref, rnorm_ref, w_t, wtemb_ref, o_ref,
                 yv, act, hid, temb_s, grp_s, sums_s, send_sem, recv_sem, loc_sem):
    me_r, me_c, peers = _me_and_peers(n_row, n_col)
    me = me_r * n_col + me_c
    n_img, hh, ww, n_ch = yv.shape
    bh, bw = hh // n_row, ww // n_col
    blk = _ResBlock(hh, ww, n_ch, rnorm_ref.at[1], w_t, act, hid, temb_s, grp_s, sums_s)
    blk.setup(temb_ref, wtemb_ref.at[1])
    _barrier(peers)

    def block(s, k, c):
        return yv.at[s, pl.ds(k * bh, bh), pl.ds(pl.multiple_of(c * bw, bw), bw), :]

    def rel(k, c):
        return lax.rem(k - me_r + n_row, n_row) * n_col + lax.rem(c - me_c + n_col, n_col)

    def copy(s, k, c):
        return pltpu.make_async_remote_copy(
            block(s, k, c), o_ref.at[me * n_img + s], send_sem.at[s, rel(k, c)], recv_sem.at[s, rel(k, c)],
            device_id={'row': k, 'col': c}, device_id_type=MESH)

    def own(s):
        return pltpu.make_async_copy(block(s, me_r, me_c), o_ref.at[me * n_img + s], loc_sem.at[s])

    def image(s, carry):
        def src(r0, n):
            return x_ref[s, r0:r0 + n]

        def dst(r0, v):
            end = r0 + v.shape[0]
            while r0 < end:
                n = min(end, (r0 // ww + 1) * ww) - r0
                yv[s, r0 // ww, r0 % ww:r0 % ww + n] = v[v.shape[0] - (end - r0):v.shape[0] - (end - r0) + n]
                r0 += n
            for k in range((end - v.shape[0]) // (bh * ww), end // (bh * ww)):
                for d in range(n_col):
                    c = lax.rem(me_c + 1 + d, n_col)
                    remote = (k != me_r) | (c != me_c)

                    @pl.when(remote)
                    def _():
                        copy(s, k, c).start()

                    @pl.when(jnp.logical_not(remote))
                    def _():
                        own(s).start()

        blk.run(src, (sums_ref[s, 0:1], sums_ref[s, 1:2]), me * n_img + s, LAST_CHUNK, dst)
        return carry

    lax.fori_loop(0, n_img, image, 0)
    for s in range(n_img):
        for r, c in peers:
            copy(s, r, c).wait()
        own(s).wait()


def _attn_kernel(x_ref, sums_ref, anorm_ref, proj_ref, o_ref, osums_ref, grp_s, k_buf, q_buf, v_buf, ot_buf):
    n_img, n_pos, n_ch = x_ref.shape
    count = float(n_pos * (n_ch // GROUPS))
    head_dim = 32
    n_heads = n_ch // head_dim
    per_blk = 128 // head_dim
    scale = LOG2E * head_dim ** -0.5

    grp_s[...] = _group_matrix(n_ch)

    def image(img, carry_img):
        sums = sums_ref[img, 0:1], sums_ref[img, 1:2]
        mean, inv = _moments(*sums, grp_s[...], count)
        a_mul = inv * anorm_ref[0:1].astype(F32)
        b_add = anorm_ref[1:2].astype(F32)
        head_rows = jnp.where(lax.broadcasted_iota(jnp.int32, (16, n_ch), 0)
                              == lax.broadcasted_iota(jnp.int32, (16, n_ch), 1) // head_dim, 1.0, 0.0).astype(BF16)

        q_top = jnp.zeros((n_heads, PROJ_TILE), F32)
        k_top = jnp.zeros((16, PROJ_TILE), F32)
        v_top = jnp.zeros((1, PROJ_TILE), F32)
        last_k = None
        for r0 in [*range(0, n_pos, PROJ_TILE), None]:
            if r0 is not None:
                tile = slice(r0, r0 + PROJ_TILE)
                g = ((x_ref[img, tile].astype(F32) - mean) * a_mul + b_add).astype(BF16)
                k = _dot(g, proj_ref[1], ((1,), (1,))).astype(BF16)
                q = _dot(proj_ref[0], g, ((1,), (1,))).astype(BF16)
                v = _dot(proj_ref[2], g, ((1,), (1,))).astype(BF16)
                k_buf[tile, :] = k
                q_buf[:, tile] = q
                v_buf[:, tile] = v
                q = q.astype(F32)
                q_top = jnp.maximum(q_top, jnp.sum((q * q).reshape(n_heads, head_dim, PROJ_TILE), axis=1))
                v_top = jnp.maximum(v_top, jnp.max(jnp.abs(v.astype(F32)), axis=0, keepdims=True))
            if last_k is not None:
                k2 = last_k.astype(F32) * last_k.astype(F32)
                k_top = jnp.maximum(k_top, _dot(head_rows, k2.astype(BF16), ((1,), (1,))))
            last_k = k

        q_top = jnp.max(q_top, axis=1, keepdims=True)
        k_top = jnp.max(k_top, axis=1, keepdims=True)[:n_heads]
        top2 = jnp.max(q_top * k_top) * (scale * scale)
        v_max = jnp.max(v_top)
        small = ((top2 < 96.0 ** 2) & (v_max < 2.0 ** 20)) | ((top2 < 108.0 ** 2) & (v_max < 2.0 ** 8))

        @pl.when(small)
        def _():
            rh = lax.broadcasted_iota(jnp.int32, (128, Q_TILE), 0) // head_dim
            n_kc = n_pos // K_CHUNK

            def heads(b, carry):
                b0 = pl.multiple_of(b * 128, 128)
                tiles = [(j, t * Q_TILE) for j in range(per_blk) for t in range(n_pos // Q_TILE)]
                steps = [(tile, c) for tile in tiles for c in range(n_kc)]
                masked = {}

                def score(step):
                    tile, c = step
                    if tile not in masked:
                        j, q0 = tile
                        masked[tile] = jnp.where(rh == j, q_buf[pl.ds(b0, 128), q0:q0 + Q_TILE], 0)
                    return _dot(k_buf[c * K_CHUNK:(c + 1) * K_CHUNK, pl.ds(b0, 128)], masked[tile])

                pending = [score(s) for s in steps[:AHEAD]]
                tot = out = None
                for n, ((j, q0), c) in enumerate(steps):
                    if n + AHEAD < len(steps):
                        pending.append(score(steps[n + AHEAD]))
                    p = jnp.exp2(pending.pop(0) * scale)
                    h0 = pl.multiple_of(b0 + j * head_dim, head_dim)
                    part = jnp.sum(p.reshape(K_CHUNK // 8, 8, Q_TILE), axis=0)
                    pv = _dot(v_buf[pl.ds(h0, head_dim), c * K_CHUNK:(c + 1) * K_CHUNK], p.astype(BF16))
                    tot, out = (part, pv) if c == 0 else (tot + part, out + pv)
                    if c == n_kc - 1:
                        res = out / jnp.sum(tot, axis=0, keepdims=True)
                        ot_buf[pl.ds(h0, head_dim), q0:q0 + Q_TILE] = res.astype(BF16)
                return carry

            lax.fori_loop(0, n_ch // 128, heads, 0)

        @pl.when(jnp.logical_not(small))
        def _():
            rh = lax.broadcasted_iota(jnp.int32, (128, 256), 0) // head_dim
            n_tiles = n_pos // 256

            def tile(i, carry):
                h = i // n_tiles
                q0 = pl.multiple_of((i % n_tiles) * 256, 256)
                b0 = pl.multiple_of((h // per_blk) * 128, 128)
                h0 = pl.multiple_of(h * head_dim, head_dim)
                qm = jnp.where(rh == h % per_blk, q_buf[pl.ds(b0, 128), pl.ds(q0, 256)], 0)
                s = _dot(k_buf[:, pl.ds(b0, 128)], qm)
                p = jnp.exp2((s - jnp.max(s, axis=0, keepdims=True)) * scale)
                o = _dot(v_buf[pl.ds(h0, head_dim), :], p.astype(BF16))
                ot_buf[pl.ds(h0, head_dim), pl.ds(q0, 256)] = (o / jnp.sum(p, axis=0, keepdims=True)).astype(BF16)
                return carry

            lax.fori_loop(0, n_heads * n_tiles, tile, 0)

        s1, s2 = _zero_sums(n_ch)
        for r0 in range(0, n_pos, PROJ_TILE):
            tile = slice(r0, r0 + PROJ_TILE)
            acc = _dot(ot_buf[:, tile], proj_ref[3], ((0,), (0,)))
            out = (x_ref[img, tile].astype(F32) + acc).astype(BF16)
            o_ref[img, tile] = out
            d1, d2 = _chan_sums(out.astype(F32))
            s1, s2 = s1 + d1, s2 + d2
        osums_ref[img, 0:1] = s1
        osums_ref[img, 1:2] = s2
        return carry_img

    lax.fori_loop(0, n_img, image, 0)


VMEM_LIMIT = 60 * 1024 * 1024


def solution(mesh):
    n_row, n_col = mesh.shape['row'], mesh.shape['col']
    n_dev = n_row * n_col
    vmem, hbm = pl.BlockSpec(memory_space=pltpu.VMEM), pl.BlockSpec(memory_space=pltpu.HBM)

    def run_stage(latent, t_emb, res_norm, res_conv, res_temb, attn_norm, attn_proj):
        n_batch, bh, bw, n_ch = latent.shape
        hh, ww = bh * n_row, bw * n_col
        n_pos, n_img = hh * ww, n_batch // n_dev
        proj = jnp.transpose(attn_proj, (0, 1, 3, 2)).reshape(4, n_ch, n_ch)
        conv_w = res_conv.reshape(2, 2, 9 * n_ch, n_ch)
        sums_shape = jax.ShapeDtypeStruct((n_img, 8, n_ch), F32)
        images = pltpu.VMEM((n_img, hh, ww, n_ch), BF16)
        work = [
            pltpu.VMEM(((hh + 2) * ww, 3 * n_ch), BF16),
            pltpu.VMEM((n_pos, n_ch), BF16),
            pltpu.VMEM((n_batch, n_ch), F32),
            pltpu.VMEM((n_ch, n_ch), BF16),
            pltpu.VMEM((8, n_ch), F32),
        ]
        remote = [pltpu.SemaphoreType.DMA((n_img, n_dev)), pltpu.SemaphoreType.DMA((n_img, n_dev)),
                  pltpu.SemaphoreType.DMA((n_img,))]

        def resident(shape, dtype=BF16):
            return pltpu.VMEM(shape, dtype)

        x1, sums1, next_w = pl.pallas_call(
            functools.partial(_first_kernel, n_row, n_col),
            out_shape=[resident((n_img, n_pos, n_ch)), resident((n_img, 8, n_ch), F32), resident((2, n_ch, 9 * n_ch))],
            in_specs=[hbm] * 5,
            out_specs=[vmem, vmem, vmem],
            scratch_shapes=[
                images, pltpu.VMEM((4, 9 * n_ch, n_ch), BF16), pltpu.VMEM((2, n_ch, 9 * n_ch), BF16),
                pltpu.VMEM(t_emb.shape, BF16), pltpu.VMEM(res_norm.shape, BF16), pltpu.VMEM(res_temb.shape[1:], BF16),
                *work, pltpu.SemaphoreType.DMA((7,)), *remote,
            ],
            compiler_params=pltpu.CompilerParams(collective_id=0, has_side_effects=True, vmem_limit_bytes=42 << 20),
        )(*(pltpu.with_memory_space_constraint(a, pltpu.HBM) for a in (latent, t_emb, res_norm, conv_w, res_temb)))

        x2, sums2 = pl.pallas_call(
            _attn_kernel,
            out_shape=[resident((n_img, n_pos, n_ch)), resident((n_img, 8, n_ch), F32)],
            in_specs=[vmem, vmem, vmem, vmem],
            out_specs=[vmem, vmem],
            scratch_shapes=[
                pltpu.VMEM((n_ch, n_ch), BF16),
                pltpu.VMEM((n_pos, n_ch), BF16),
                pltpu.VMEM((n_ch, n_pos), BF16),
                pltpu.VMEM((n_ch, n_pos), BF16),
                pltpu.VMEM((n_ch, n_pos), BF16),
            ],
            compiler_params=pltpu.CompilerParams(vmem_limit_bytes=24 << 20),
        )(x1, sums1, attn_norm, proj)

        return pl.pallas_call(
            functools.partial(_last_kernel, n_row, n_col),
            out_shape=resident(latent.shape),
            in_specs=[vmem] * 6,
            out_specs=vmem,
            scratch_shapes=[images, *work, *remote],
            compiler_params=pltpu.CompilerParams(collective_id=1, has_side_effects=True, vmem_limit_bytes=24 << 20),
        )(x2, sums2, t_emb, res_norm, next_w, res_temb)

    spec_x = P('dp', 'row', 'col', None)
    return jax.shard_map(run_stage, mesh=mesh, in_specs=(spec_x, P('dp', None), P(), P(), P(), P(), P()), out_specs=spec_x, check_vma=False)
```

profile of v0, /device:TPU:1, one launch (start us, length us, event | category | flops | bytes accessed | tf_op | source)
XLA Modules:
  0.0 175.5 jit_solution(17981693737809906887)
XLA Ops:
  0.0 0.0 copy-start.1
  0.0 0.0 copy-start.4
  0.0 41.2 %shard_map.73 = (bf16[2,1536,384]{2,1,0:T(8,128)(2,1)S(1)}, f32[2,8,384]{2,1,0:T(8,128)S(1)}, bf16[2,384,3456]{2,1,0:T(8,128)(2,1)S(1)}) custom-call(bf16[16,4,48,384]{3,2,1,0:T(8,128)(2,1)} %lat_ref.1, bf16[16,768]{1,0:T(8,128)(2,1)} %temb_ref.1, bf16[2,2,2,384]{3,2,1,0:T(2,128)(2,1)} %rnorm_ref.1, bf16[2,2,3456,384]{3,2,1,0:T(8,128)(2,1)} %bitcast.5, ...), custom_call_target="tpu_custom_call" | custom-call | tf_op jit(solution)/shard_map/pallas_call | solution.py:419
  41.2 0.0 copy-start
  41.2 0.0 copy-start.2
  41.3 0.0 copy-start.3
  41.3 0.0 copy-done.1
  41.3 0.0 copy-done.4
  41.3 54.1 %shard_map.74 = (bf16[2,1536,384]{2,1,0:T(8,128)(2,1)S(1)}, f32[2,8,384]{2,1,0:T(8,128)S(1)}) custom-call(bf16[2,1536,384]{2,1,0:T(8,128)(2,1)S(1)} %get-tuple-element.10.x_ref, f32[2,8,384]{2,1,0:T(8,128)S(1)} %get-tuple-element.11.sums_ref, bf16[2,384]{1,0:T(2,128)(2,1)S(1)} %copy-done.4, bf16[4,384,384]{2,1,0:T(8,128)(2,1)S(1)} %bitcast.4), custom_call_target="tpu_custom_call" | custom-call | tf_op jit(solution)/shard_map/pallas_call | solution.py:432
  95.4 0.0 copy-done
  95.4 0.0 copy-done.2
  95.4 0.0 copy-done.3
  95.4 78.7 %shard_map.75 = bf16[16,4,48,384]{3,2,1,0:T(8,128)(2,1)S(1)} custom-call(bf16[2,1536,384]{2,1,0:T(8,128)(2,1)S(1)} %get-tuple-element.12.x_ref, f32[2,8,384]{2,1,0:T(8,128)S(1)} %get-tuple-element.13.sums_ref, bf16[16,768]{1,0:T(8,128)(2,1)S(1)} %copy-done.2, bf16[2,2,2,384]{3,2,1,0:T(2,128)(2,1)S(1)} %copy-done.3, ...), custom_call_target="tpu_custom_call" | custom-call | tf_op jit(solution)/shard_map/pallas_call | solution.py:447
  174.1 1.4 copy.9
Async XLA Ops:
  0.0 41.3 %copy-start.1 = (bf16[4,12,384,32]{2,3,1,0:T(8,128)(2,1)S(1)}, bf16[4,12,384,32]{2,3,1,0:T(8,128)(2,1)}, u32[]{:S(2)}) copy-start(bf16[4,12,384,32]{2,3,1,0:T(8,128)(2,1)} %param.13) | copy-start | bytes 3538948
  0.0 41.3 %copy-start.4 = (bf16[2,384]{1,0:T(2,128)(2,1)S(1)}, bf16[2,384]{1,0:T(2,128)(2,1)}, u32[]{:S(2)}) copy-start(bf16[2,384]{1,0:T(2,128)(2,1)} %anorm_ref.1) | copy-start | bytes 4612
  41.2 54.2 %copy-start = (bf16[2,768,384]{2,1,0:T(8,128)(2,1)S(1)}, bf16[2,768,384]{2,1,0:T(8,128)(2,1)}, u32[]{:S(2)}) copy-start(bf16[2,768,384]{2,1,0:T(8,128)(2,1)} %wtemb_ref.1) | copy-start | bytes 3538948
  41.2 54.2 %copy-start.2 = (bf16[16,768]{1,0:T(8,128)(2,1)S(1)}, bf16[16,768]{1,0:T(8,128)(2,1)}, u32[]{:S(2)}) copy-start(bf16[16,768]{1,0:T(8,128)(2,1)} %temb_ref.1) | copy-start | bytes 73732
  41.3 54.2 %copy-start.3 = (bf16[2,2,2,384]{3,2,1,0:T(2,128)(2,1)S(1)}, bf16[2,2,2,384]{3,2,1,0:T(2,128)(2,1)}, u32[]{:S(2)}) copy-start(bf16[2,2,2,384]{3,2,1,0:T(2,128)(2,1)} %rnorm_ref.1) | copy-start | bytes 18436
where the time goes:
time: 176 us
  Pallas kernels  174 us (99%)
    pallas_call x1, Pallas kernels, run_stage(): pl.pallas_call(functools.partial(_last_kernel, n_row, n_col), out_shape=r...  78.7 us
    pallas_call x1, Pallas kernels, run_stage(): pl.pallas_call(_attn_kernel, out_shape=[resident((n_img, n_pos, n_ch)), r...  54.1 us
    pallas_call x1, Pallas kernels, run_stage(): pl.pallas_call(functools.partial(_first_kernel, n_row, n_col), out_shape=...  41.2 us

commit v1 on v0

--- a/solution.py
+++ b/solution.py
@@ -58,7 +58,8 @@
     r1 = st - hi.astype(F32)
     mid = r1.astype(BF16)
     lo = (r1 - mid.astype(F32)).astype(BF16)
-    tot = (_dot(lo, grp) + _dot(mid, grp)) + _dot(hi, grp)
+    parts = _dot(jnp.concatenate([hi.astype(F32), mid.astype(F32), lo.astype(F32)], axis=0).astype(BF16), grp)
+    tot = (parts[16:24] + parts[8:16]) + parts[0:8]
     mean = tot[0:1] / count
     var = tot[1:2] / count - mean * mean
     return mean, lax.rsqrt(var + EPS)
@@ -84,7 +85,7 @@
         self.act[0:self.ww, :] = zeros
         self.act[(self.hh + 1) * self.ww:(self.hh + 2) * self.ww, :] = zeros
 
-    def conv(self, j, src, sums, chunk, epilogue):
+    def conv(self, j, src, sums, chunk, epilogue, backward=False):
         ww, n_ch, act = self.ww, self.n_ch, self.act
         mean, inv = _moments(*sums, self.grp_s[...], self.count)
         a_mul = inv * self.rnorm_ref[j, 0:1].astype(F32)
@@ -101,25 +102,29 @@
             act[d0:d0 + ww, n_ch:2 * n_ch] = a.astype(BF16)
             act[d0:d0 + ww, 2 * n_ch:3 * n_ch] = right.astype(BF16)
 
-        def need(n):
-            return min(self.hh, -(-(n + ww) // ww))
-
-        n_pos = self.hh * ww
-        for i in range(need(chunk)):
-            fill(i)
+        n_pos, filled = self.hh * ww, set()
+
+        def fill_for(r0):
+            for i in range(max(0, r0 // ww - 1), min(self.hh, (r0 + chunk - 1) // ww + 2)):
+                if i not in filled:
+                    filled.add(i)
+                    fill(i)
+
+        starts = list(range(0, n_pos, chunk))[::-1 if backward else 1]
+        fill_for(starts[0])
         s1, s2 = _zero_sums(n_ch)
-        for r0 in range(0, n_pos, chunk):
+        for at, r0 in enumerate(starts):
             lhs = jnp.concatenate([act[r0 + dy * ww:r0 + dy * ww + chunk, :] for dy in range(3)], axis=1)
             acc = _dot(self.w_t[j], lhs, ((1,), (1,)))
-            for i in range(need(r0 + chunk), need(min(n_pos, r0 + 2 * chunk))):
-                fill(i)
+            for ahead in starts[at + 1:at + 2]:
+                fill_for(ahead)
             out = epilogue(r0, acc.T)
             d1, d2 = _chan_sums(out.astype(F32))
             s1, s2 = s1 + d1, s2 + d2
         self.sums_s[0:1] = s1
         self.sums_s[1:2] = s2
 
-    def run(self, src, sums, img, last_chunk, dst):
+    def run(self, src, sums, img, last_chunk, dst, backward=None):
         hid, sums_s = self.hid, self.sums_s
         t_row = self.temb_s[pl.ds(img, 1), :]
 
@@ -135,9 +140,14 @@
 
         self.conv(0, src, sums, CHUNK, first)
 
-        @pl.when(img >= 0)
-        def _():
-            self.conv(1, lambda r0, n: hid[r0:r0 + n], (sums_s[0:1], sums_s[1:2]), last_chunk, second)
+        def last(order):
+            self.conv(1, lambda r0, n: hid[r0:r0 + n], (sums_s[0:1], sums_s[1:2]), last_chunk, second, order)
+
+        if backward is None:
+            pl.when(img >= 0)(lambda: last(False))
+        else:
+            pl.when(backward)(lambda: last(True))
+            pl.when(jnp.logical_not(backward))(lambda: last(False))
 
 
 def _first_kernel(n_row, n_col, lat_ref, temb_hbm, rnorm_hbm, conv_hbm, wtemb_hbm, o_ref, sums_ref, next_w,
@@ -243,13 +253,25 @@
         def src(r0, n):
             return x_ref[s, r0:r0 + n]
 
+        def ready(r0, end):
+            size, blocks = bh * ww, []
+            for k in range(n_row):
+                if k * size < end and (k + 1) * size > r0:
+                    done.setdefault(k, set()).update(range(max(r0, k * size), min(end, (k + 1) * size)))
+                    if len(done[k]) == size:
+                        done.pop(k)
+                        blocks.append(k)
+            return blocks
+
+        done = {}
+
         def dst(r0, v):
-            end = r0 + v.shape[0]
-            while r0 < end:
-                n = min(end, (r0 // ww + 1) * ww) - r0
-                yv[s, r0 // ww, r0 % ww:r0 % ww + n] = v[v.shape[0] - (end - r0):v.shape[0] - (end - r0) + n]
-                r0 += n
-            for k in range((end - v.shape[0]) // (bh * ww), end // (bh * ww)):
+            end, at = r0 + v.shape[0], r0
+            while at < end:
+                n = min(end, (at // ww + 1) * ww) - at
+                yv[s, at // ww, at % ww:at % ww + n] = v[at - r0:at - r0 + n]
+                at += n
+            for k in ready(r0, end):
                 for d in range(n_col):
                     c = lax.rem(me_c + 1 + d, n_col)
                     remote = (k != me_r) | (c != me_c)
@@ -262,7 +284,7 @@
                     def _():
                         own(s).start()
 
-        blk.run(src, (sums_ref[s, 0:1], sums_ref[s, 1:2]), me * n_img + s, LAST_CHUNK, dst)
+        blk.run(src, (sums_ref[s, 0:1], sums_ref[s, 1:2]), me * n_img + s, LAST_CHUNK, dst, me_r < n_row // 2)
         return carry
 
     lax.fori_loop(0, n_img, image, 0)

time: 176 us -> 175 us (level)
  Pallas kernels: 174 us -> 171 us
    pallas_call x1, Pallas kernels: 78.7 us -> 76.5 us  [run_stage(): pl.pallas_call(functools.partial(_last_kernel, n_row, n_col), out_shape=r...]
where the time goes in v1:
time: 175 us; the launch traced here: 173 us
  Pallas kernels  171 us (98%)
    pallas_call x1, Pallas kernels, run_stage(): pl.pallas_call(functools.partial(_last_kernel, n_row, n_col), out_shape=r...  76.5 us
    pallas_call x1, Pallas kernels, run_stage(): pl.pallas_call(_attn_kernel, out_shape=[resident((n_img, n_pos, n_ch)), r...  53.9 us
    pallas_call x1, Pallas kernels, run_stage(): pl.pallas_call(functools.partial(_first_kernel, n_row, n_col), out_shape=...  41 us

profile of v1, /device:TPU:1, one launch (start us, length us, event | category | flops | bytes accessed | tf_op | source)
XLA Modules:
  0.0 172.9 jit_solution(1939376341430460219)
XLA Ops:
  0.0 0.0 copy-start.1
  0.0 0.0 copy-start.4
  0.0 41.0 %shard_map.73 = (bf16[2,1536,384]{2,1,0:T(8,128)(2,1)S(1)}, f32[2,8,384]{2,1,0:T(8,128)S(1)}, bf16[2,384,3456]{2,1,0:T(8,128)(2,1)S(1)}) custom-call(bf16[16,4,48,384]{3,2,1,0:T(8,128)(2,1)} %lat_ref.1, bf16[16,768]{1,0:T(8,128)(2,1)} %temb_ref.1, bf16[2,2,2,384]{3,2,1,0:T(2,128)(2,1)} %rnorm_ref.1, bf16[2,2,3456,384]{3,2,1,0:T(8,128)(2,1)} %bitcast.5, ...), custom_call_target="tpu_custom_call" | custom-call | tf_op jit(solution)/shard_map/pallas_call | solution.py:441
  41.1 0.0 copy-start
  41.1 0.0 copy-start.2
  41.1 0.0 copy-start.3
  41.1 0.0 copy-done.1
  41.1 0.0 copy-done.4
  41.1 53.9 %shard_map.74 = (bf16[2,1536,384]{2,1,0:T(8,128)(2,1)S(1)}, f32[2,8,384]{2,1,0:T(8,128)S(1)}) custom-call(bf16[2,1536,384]{2,1,0:T(8,128)(2,1)S(1)} %get-tuple-element.10.x_ref, f32[2,8,384]{2,1,0:T(8,128)S(1)} %get-tuple-element.11.sums_ref, bf16[2,384]{1,0:T(2,128)(2,1)S(1)} %copy-done.4, bf16[4,384,384]{2,1,0:T(8,128)(2,1)S(1)} %bitcast.4), custom_call_target="tpu_custom_call" | custom-call | tf_op jit(solution)/shard_map/pallas_call | solution.py:454
  95.0 0.0 copy-done
  95.0 0.0 copy-done.2
  95.0 0.0 copy-done.3
  95.0 76.5 %shard_map.75 = bf16[16,4,48,384]{3,2,1,0:T(8,128)(2,1)S(1)} custom-call(bf16[2,1536,384]{2,1,0:T(8,128)(2,1)S(1)} %get-tuple-element.12.x_ref, f32[2,8,384]{2,1,0:T(8,128)S(1)} %get-tuple-element.13.sums_ref, bf16[16,768]{1,0:T(8,128)(2,1)S(1)} %copy-done.2, bf16[2,2,2,384]{3,2,1,0:T(2,128)(2,1)S(1)} %copy-done.3, ...), custom_call_target="tpu_custom_call" | custom-call | tf_op jit(solution)/shard_map/pallas_call | solution.py:469
  171.5 1.4 copy.9
Async XLA Ops:
  0.0 41.1 %copy-start.1 = (bf16[4,12,384,32]{2,3,1,0:T(8,128)(2,1)S(1)}, bf16[4,12,384,32]{2,3,1,0:T(8,128)(2,1)}, u32[]{:S(2)}) copy-start(bf16[4,12,384,32]{2,3,1,0:T(8,128)(2,1)} %param.13) | copy-start | bytes 3538948
  0.0 41.1 %copy-start.4 = (bf16[2,384]{1,0:T(2,128)(2,1)S(1)}, bf16[2,384]{1,0:T(2,128)(2,1)}, u32[]{:S(2)}) copy-start(bf16[2,384]{1,0:T(2,128)(2,1)} %anorm_ref.1) | copy-start | bytes 4612
  41.1 53.9 %copy-start = (bf16[2,768,384]{2,1,0:T(8,128)(2,1)S(1)}, bf16[2,768,384]{2,1,0:T(8,128)(2,1)}, u32[]{:S(2)}) copy-start(bf16[2,768,384]{2,1,0:T(8,128)(2,1)} %wtemb_ref.1) | copy-start | bytes 3538948
  41.1 53.9 %copy-start.2 = (bf16[16,768]{1,0:T(8,128)(2,1)S(1)}, bf16[16,768]{1,0:T(8,128)(2,1)}, u32[]{:S(2)}) copy-start(bf16[16,768]{1,0:T(8,128)(2,1)} %temb_ref.1) | copy-start | bytes 73732
  41.1 53.9 %copy-start.3 = (bf16[2,2,2,384]{3,2,1,0:T(2,128)(2,1)S(1)}, bf16[2,2,2,384]{3,2,1,0:T(2,128)(2,1)}, u32[]{:S(2)}) copy-start(bf16[2,2,2,384]{3,2,1,0:T(2,128)(2,1)} %rnorm_ref.1) | copy-start | bytes 18436

commit v2 on v1

--- a/solution.py
+++ b/solution.py
@@ -23,10 +23,14 @@
 
 def _me_and_peers(n_row, n_col):
     me_r, me_c = lax.axis_index('row'), lax.axis_index('col')
-    peers = []
-    for k in range(1, n_row * n_col):
-        peers.append((lax.rem(me_r + k // n_col, n_row), lax.rem(me_c + k % n_col, n_col)))
-    return me_r, me_c, peers
+    half = n_row // 2
+
+    def other(r, far, core):
+        r = lax.rem(r + far * half, n_row)
+        return r // half * half + lax.rem(lax.rem(r, half) + core, half)
+
+    order = [(f, k, c) for f, c in ((1, 1), (1, 0), (0, 1), (0, 0)) for k in range(half) if f or c or k]
+    return me_r, me_c, [(other(me_r, f, k), lax.rem(me_c + c, n_col)) for f, k, c in order]
 
 
 def _barrier(peers):
@@ -89,18 +93,19 @@
         ww, n_ch, act = self.ww, self.n_ch, self.act
         mean, inv = _moments(*sums, self.grp_s[...], self.count)
         a_mul = inv * self.rnorm_ref[j, 0:1].astype(F32)
-        b_add = self.rnorm_ref[j, 1:2].astype(F32)
-        col = lax.broadcasted_iota(jnp.int32, (ww, 1), 0)
+        half_b = 0.5 * (self.rnorm_ref[j, 1:2].astype(F32) - mean * a_mul)
+        half_a = 0.5 * a_mul
+        edge = jnp.zeros((1, n_ch), BF16)
 
         def fill(i):
-            u = (src(i * ww, ww).astype(F32) - mean) * a_mul + b_add
-            a = u * (0.5 * jnp.tanh(0.5 * u) + 0.5)
-            left = jnp.where(col == 0, 0.0, pltpu.roll(a, 1, 0))
-            right = jnp.where(col == ww - 1, 0.0, pltpu.roll(a, ww - 1, 0))
+            w = src(i * ww, ww).astype(F32) * half_a + half_b
+            a = w * jnp.tanh(w) + w
             d0 = (i + 1) * ww
-            act[d0:d0 + ww, 0:n_ch] = left.astype(BF16)
+            act[d0:d0 + ww, 0:n_ch] = pltpu.roll(a, 1, 0).astype(BF16)
             act[d0:d0 + ww, n_ch:2 * n_ch] = a.astype(BF16)
-            act[d0:d0 + ww, 2 * n_ch:3 * n_ch] = right.astype(BF16)
+            act[d0:d0 + ww, 2 * n_ch:3 * n_ch] = pltpu.roll(a, ww - 1, 0).astype(BF16)
+            act[d0:d0 + 1, 0:n_ch] = edge
+            act[d0 + ww - 1:d0 + ww, 2 * n_ch:3 * n_ch] = edge
 
         n_pos, filled = self.hh * ww, set()
 
@@ -320,10 +325,15 @@
             if r0 is not None:
                 tile = slice(r0, r0 + PROJ_TILE)
                 g = ((x_ref[img, tile].astype(F32) - mean) * a_mul + b_add).astype(BF16)
-                k = _dot(g, proj_ref[1], ((1,), (1,))).astype(BF16)
+                k = _dot(g, proj_ref[1], ((1,), (1,)))
                 q = _dot(proj_ref[0], g, ((1,), (1,))).astype(BF16)
                 v = _dot(proj_ref[2], g, ((1,), (1,))).astype(BF16)
-                k_buf[tile, :] = k
+                for b0 in range(0, n_ch, 128):
+                    for j in range(per_blk):
+                        part = k[:, b0:b0 + 128]
+                        part = part if j == 0 else pltpu.roll(part, 128 - j * head_dim, 1)
+                        k_buf[j, tile, b0:b0 + 128] = part.astype(BF16)
+                k = k.astype(BF16)
                 q_buf[:, tile] = q
                 v_buf[:, tile] = v
                 q = q.astype(F32)
@@ -342,21 +352,18 @@
 
         @pl.when(small)
         def _():
-            rh = lax.broadcasted_iota(jnp.int32, (128, Q_TILE), 0) // head_dim
             n_kc = n_pos // K_CHUNK
 
             def heads(b, carry):
                 b0 = pl.multiple_of(b * 128, 128)
                 tiles = [(j, t * Q_TILE) for j in range(per_blk) for t in range(n_pos // Q_TILE)]
                 steps = [(tile, c) for tile in tiles for c in range(n_kc)]
-                masked = {}
 
                 def score(step):
-                    tile, c = step
-                    if tile not in masked:
-                        j, q0 = tile
-                        masked[tile] = jnp.where(rh == j, q_buf[pl.ds(b0, 128), q0:q0 + Q_TILE], 0)
-                    return _dot(k_buf[c * K_CHUNK:(c + 1) * K_CHUNK, pl.ds(b0, 128)], masked[tile])
+                    (j, q0), c = step
+                    h0 = pl.multiple_of(b0 + j * head_dim, head_dim)
+                    keys = k_buf[j, c * K_CHUNK:(c + 1) * K_CHUNK, pl.ds(b0, 128)]
+                    return _dot(keys[:, :head_dim], q_buf[pl.ds(h0, head_dim), q0:q0 + Q_TILE])
 
                 pending = [score(s) for s in steps[:AHEAD]]
                 tot = out = None
@@ -386,7 +393,7 @@
                 b0 = pl.multiple_of((h // per_blk) * 128, 128)
                 h0 = pl.multiple_of(h * head_dim, head_dim)
                 qm = jnp.where(rh == h % per_blk, q_buf[pl.ds(b0, 128), pl.ds(q0, 256)], 0)
-                s = _dot(k_buf[:, pl.ds(b0, 128)], qm)
+                s = _dot(k_buf[0, :, pl.ds(b0, 128)], qm)
                 p = jnp.exp2((s - jnp.max(s, axis=0, keepdims=True)) * scale)
                 o = _dot(v_buf[pl.ds(h0, head_dim), :], p.astype(BF16))
                 ot_buf[pl.ds(h0, head_dim), pl.ds(q0, 256)] = (o / jnp.sum(p, axis=0, keepdims=True)).astype(BF16)
@@ -458,7 +465,7 @@
             out_specs=[vmem, vmem],
             scratch_shapes=[
                 pltpu.VMEM((n_ch, n_ch), BF16),
-                pltpu.VMEM((n_pos, n_ch), BF16),
+                pltpu.VMEM((4, n_pos, n_ch), BF16),
                 pltpu.VMEM((n_ch, n_pos), BF16),
                 pltpu.VMEM((n_ch, n_pos), BF16),
                 pltpu.VMEM((n_ch, n_pos), BF16),

time: 175 us -> 173 us (0.989); the launches traced: 173 us -> 173 us
    pallas_call x1, Pallas kernels: 53.9 us -> 94.1 us  [run_stage(): pl.pallas_call(_attn_kernel, out_shape=[resident((n_img, n_pos, n_ch)), r...]
    pallas_call x1, Pallas kernels: 76.5 us -> 36.8 us  [run_stage(): pl.pallas_call(functools.partial(_last_kernel, n_row, n_col), out_shape=r...]
where the time goes in v2:
time: 173 us
  Pallas kernels  172 us (99%)
    pallas_call x1, Pallas kernels, run_stage(): pl.pallas_call(_attn_kernel, out_shape=[resident((n_img, n_pos, n_ch)), r...  94.1 us
    pallas_call x1, Pallas kernels, run_stage(): pl.pallas_call(functools.partial(_first_kernel, n_row, n_col), out_shape=...  41 us
    pallas_call x1, Pallas kernels, run_stage(): pl.pallas_call(functools.partial(_last_kernel, n_row, n_col), out_shape=r...  36.8 us

profile of v2, /device:TPU:1, one launch (start us, length us, event | category | flops | bytes accessed | tf_op | source)
XLA Modules:
  0.0 173.4 jit_solution(5513949532889466399)
XLA Ops:
  0.0 0.0 copy-start.1
  0.0 0.0 copy-start.4
  0.0 41.0 %shard_map.73 = (bf16[2,1536,384]{2,1,0:T(8,128)(2,1)S(1)}, f32[2,8,384]{2,1,0:T(8,128)S(1)}, bf16[2,384,3456]{2,1,0:T(8,128)(2,1)S(1)}) custom-call(bf16[16,4,48,384]{3,2,1,0:T(8,128)(2,1)} %lat_ref.1, bf16[16,768]{1,0:T(8,128)(2,1)} %temb_ref.1, bf16[2,2,2,384]{3,2,1,0:T(2,128)(2,1)} %rnorm_ref.1, bf16[2,2,3456,384]{3,2,1,0:T(8,128)(2,1)} %bitcast.5, ...), custom_call_target="tpu_custom_call" | custom-call | tf_op jit(solution)/shard_map/pallas_call | solution.py:448
  41.0 0.0 copy-start
  41.0 0.0 copy-start.2
  41.0 0.0 copy-start.3
  41.0 0.0 copy-done.1
  41.0 0.0 copy-done.4
  41.0 94.1 %shard_map.74 = (bf16[2,1536,384]{2,1,0:T(8,128)(2,1)S(1)}, f32[2,8,384]{2,1,0:T(8,128)S(1)}) custom-call(bf16[2,1536,384]{2,1,0:T(8,128)(2,1)S(1)} %get-tuple-element.10.x_ref, f32[2,8,384]{2,1,0:T(8,128)S(1)} %get-tuple-element.11.sums_ref, bf16[2,384]{1,0:T(2,128)(2,1)S(1)} %copy-done.4, bf16[4,384,384]{2,1,0:T(8,128)(2,1)S(1)} %bitcast.4), custom_call_target="tpu_custom_call" | custom-call | tf_op jit(solution)/shard_map/pallas_call | solution.py:461
  135.2 0.0 copy-done
  135.2 0.0 copy-done.2
  135.2 0.0 copy-done.3
  135.2 36.8 %shard_map.75 = bf16[16,4,48,384]{3,2,1,0:T(8,128)(2,1)S(1)} custom-call(bf16[2,1536,384]{2,1,0:T(8,128)(2,1)S(1)} %get-tuple-element.12.x_ref, f32[2,8,384]{2,1,0:T(8,128)S(1)} %get-tuple-element.13.sums_ref, bf16[16,768]{1,0:T(8,128)(2,1)S(1)} %copy-done.2, bf16[2,2,2,384]{3,2,1,0:T(2,128)(2,1)S(1)} %copy-done.3, ...), custom_call_target="tpu_custom_call" | custom-call | tf_op jit(solution)/shard_map/pallas_call | solution.py:476
  172.0 1.4 copy.9
Async XLA Ops:
  0.0 41.0 %copy-start.1 = (bf16[4,12,384,32]{2,3,1,0:T(8,128)(2,1)S(1)}, bf16[4,12,384,32]{2,3,1,0:T(8,128)(2,1)}, u32[]{:S(2)}) copy-start(bf16[4,12,384,32]{2,3,1,0:T(8,128)(2,1)} %param.13) | copy-start | bytes 3538948
  0.0 41.0 %copy-start.4 = (bf16[2,384]{1,0:T(2,128)(2,1)S(1)}, bf16[2,384]{1,0:T(2,128)(2,1)}, u32[]{:S(2)}) copy-start(bf16[2,384]{1,0:T(2,128)(2,1)} %anorm_ref.1) | copy-start | bytes 4612
  41.0 94.2 %copy-start = (bf16[2,768,384]{2,1,0:T(8,128)(2,1)S(1)}, bf16[2,768,384]{2,1,0:T(8,128)(2,1)}, u32[]{:S(2)}) copy-start(bf16[2,768,384]{2,1,0:T(8,128)(2,1)} %wtemb_ref.1) | copy-start | bytes 3538948
  41.0 94.2 %copy-start.2 = (bf16[16,768]{1,0:T(8,128)(2,1)S(1)}, bf16[16,768]{1,0:T(8,128)(2,1)}, u32[]{:S(2)}) copy-start(bf16[16,768]{1,0:T(8,128)(2,1)} %temb_ref.1) | copy-start | bytes 73732
  41.0 94.2 %copy-start.3 = (bf16[2,2,2,384]{3,2,1,0:T(2,128)(2,1)S(1)}, bf16[2,2,2,384]{3,2,1,0:T(2,128)(2,1)}, u32[]{:S(2)}) copy-start(bf16[2,2,2,384]{3,2,1,0:T(2,128)(2,1)} %rnorm_ref.1) | copy-start | bytes 18436

commit v3 on v2

--- a/solution.py
+++ b/solution.py
@@ -80,11 +80,7 @@
         self.temb_s, self.grp_s, self.sums_s = temb_s, grp_s, sums_s
         self.count = float(hh * ww * (n_ch // GROUPS))
 
-    def setup(self, temb_ref, wtemb_ref):
-        te = temb_ref[...].astype(F32)
-        t_act = (te * jax.nn.sigmoid(te)).astype(BF16)
-        self.temb_s[...] = _dot(t_act, wtemb_ref[...])
-        self.grp_s[...] = _group_matrix(self.n_ch)
+    def clear_borders(self):
         zeros = jnp.zeros((self.ww, self.act.shape[1]), BF16)
         self.act[0:self.ww, :] = zeros
         self.act[(self.hh + 1) * self.ww:(self.hh + 2) * self.ww, :] = zeros
@@ -129,7 +125,7 @@
         self.sums_s[0:1] = s1
         self.sums_s[1:2] = s2
 
-    def run(self, src, sums, img, last_chunk, dst, backward=None):
+    def run(self, src, sums, img, last_chunk, dst, backward):
         hid, sums_s = self.hid, self.sums_s
         t_row = self.temb_s[pl.ds(img, 1), :]
 
@@ -148,25 +144,67 @@
         def last(order):
             self.conv(1, lambda r0, n: hid[r0:r0 + n], (sums_s[0:1], sums_s[1:2]), last_chunk, second, order)
 
-        if backward is None:
-            pl.when(img >= 0)(lambda: last(False))
-        else:
-            pl.when(backward)(lambda: last(True))
-            pl.when(jnp.logical_not(backward))(lambda: last(False))
-
-
-def _first_kernel(n_row, n_col, lat_ref, temb_hbm, rnorm_hbm, conv_hbm, wtemb_hbm, o_ref, sums_ref, next_w,
-                  xv, wconv, w_t, temb_v, rnorm_v, wtemb, act, hid, temb_s, grp_s, sums_s, wsem, send_sem, recv_sem, loc_sem):
+        pl.when(backward)(lambda: last(True))
+        pl.when(jnp.logical_not(backward))(lambda: last(False))
+
+
+HEAD_DIM = 32
+LOGIT_SCALE = LOG2E * HEAD_DIM ** -0.5
+
+
+def _project(src, n_pos, sums, grp, anorm_ref, proj_ref, k_buf, q_buf, v_buf, bound_ref):
+    n_ch = proj_ref.shape[-1]
+    n_heads = n_ch // HEAD_DIM
+    mean, inv = _moments(*sums, grp, float(n_pos * (n_ch // GROUPS)))
+    a_mul = inv * anorm_ref[0:1].astype(F32)
+    b_add = anorm_ref[1:2].astype(F32)
+    head_rows = jnp.where(lax.broadcasted_iota(jnp.int32, (16, n_ch), 0)
+                          == lax.broadcasted_iota(jnp.int32, (16, n_ch), 1) // HEAD_DIM, 1.0, 0.0).astype(BF16)
+    q_top = jnp.zeros((n_heads, PROJ_TILE), F32)
+    k_top = jnp.zeros((16, PROJ_TILE), F32)
+    v_top = jnp.zeros((1, PROJ_TILE), F32)
+    last_k = None
+    for r0 in [*range(0, n_pos, PROJ_TILE), None]:
+        if r0 is not None:
+            tile = slice(r0, r0 + PROJ_TILE)
+            g = ((src(r0, PROJ_TILE).astype(F32) - mean) * a_mul + b_add).astype(BF16)
+            k = _dot(g, proj_ref[1], ((1,), (1,)))
+            q = _dot(proj_ref[0], g, ((1,), (1,))).astype(BF16)
+            v = _dot(proj_ref[2], g, ((1,), (1,))).astype(BF16)
+            for b0 in range(0, n_ch, 128):
+                for j in range(128 // HEAD_DIM):
+                    part = k[:, b0:b0 + 128]
+                    part = part if j == 0 else pltpu.roll(part, 128 - j * HEAD_DIM, 1)
+                    k_buf[j, tile, b0:b0 + 128] = part.astype(BF16)
+            k = k.astype(BF16)
+            q_buf[:, tile] = q
+            v_buf[:, tile] = v
+            q = q.astype(F32)
+            q_top = jnp.maximum(q_top, jnp.sum((q * q).reshape(n_heads, HEAD_DIM, PROJ_TILE), axis=1))
+            v_top = jnp.maximum(v_top, jnp.max(jnp.abs(v.astype(F32)), axis=0, keepdims=True))
+        if last_k is not None:
+            k2 = last_k.astype(F32) * last_k.astype(F32)
+            k_top = jnp.maximum(k_top, _dot(head_rows, k2.astype(BF16), ((1,), (1,))))
+        last_k = k
+    q_top = jnp.max(q_top, axis=1, keepdims=True)
+    k_top = jnp.max(k_top, axis=1, keepdims=True)[:n_heads]
+    top2 = jnp.max(q_top * k_top, axis=0, keepdims=True) * (LOGIT_SCALE * LOGIT_SCALE)
+    bound_ref[0:1] = jnp.broadcast_to(top2, (1, 128))
+    bound_ref[1:2] = jnp.broadcast_to(jnp.max(v_top, axis=1, keepdims=True), (1, 128))
+
+
+def _first_kernel(n_row, n_col, lat_ref, temb_hbm, rnorm_hbm, conv_hbm, wtemb_hbm, anorm_hbm, proj_hbm,
+                  o_ref, sums_ref, next_w, next_temb, grp_ref, k_buf, q_buf, v_buf, bound_ref,
+                  xv, wconv, w_t, temb_v, rnorm_v, wtemb, anorm_v, proj_v, act, temb_s, sums_s,
+                  wsem, send_sem, recv_sem, loc_sem):
     me_r, me_c, peers = _me_and_peers(n_row, n_col)
     me = me_r * n_col + me_c
     n_img, hh, ww, n_ch = xv.shape
+    n_pos = hh * ww
     bh, bw = hh // n_row, ww // n_col
     weights = [pltpu.make_async_copy(conv_hbm.at[i // 2, i % 2], wconv.at[i], wsem.at[i]) for i in range(4)]
-    small = [
-        pltpu.make_async_copy(wtemb_hbm.at[0], wtemb, wsem.at[4]),
-        pltpu.make_async_copy(temb_hbm, temb_v, wsem.at[5]),
-        pltpu.make_async_copy(rnorm_hbm, rnorm_v, wsem.at[6]),
-    ]
+    small = [pltpu.make_async_copy(a, b, wsem.at[4 + i]) for i, (a, b) in enumerate([
+        (wtemb_hbm, wtemb), (temb_hbm, temb_v), (rnorm_hbm, rnorm_v), (anorm_hbm, anorm_v), (proj_hbm, proj_v)])]
 
     def place(s):
         return xv.at[s, pl.ds(me_r * bh, bh), pl.ds(pl.multiple_of(me_c * bw, bw), bw), :]
@@ -188,10 +226,15 @@
     for w in [*small, *weights]:
         w.start()
 
-    blk = _ResBlock(hh, ww, n_ch, rnorm_v.at[0], w_t, act, hid, temb_s, grp_s, sums_s)
+    blk = _ResBlock(hh, ww, n_ch, rnorm_v.at[0], w_t, act, None, temb_s, grp_ref, sums_s)
+    blk.clear_borders()
+    grp_ref[...] = _group_matrix(n_ch)
     for w in small:
         w.wait()
-    blk.setup(temb_v, wtemb)
+    te = temb_v[...].astype(F32)
+    t_act = (te * jax.nn.sigmoid(te)).astype(BF16)
+    temb_s[...] = _dot(t_act, wtemb[0])
+    next_temb[...] = _dot(t_act, wtemb[1])
     for w in weights:
         w.wait()
 
@@ -204,40 +247,57 @@
 
     lax.fori_loop(0, 9, turn, 0)
 
-    def image(s, carry):
-        for k in range(len(peers)):
-            copy(s, k).wait_recv()
-        own(s).wait()
-
-        def src(r0, n):
-            return xv[s, pl.ds(r0 // ww, n // ww)].reshape(n, n_ch)
-
-        def in_sums(i, sums):
-            d1, d2 = _chan_sums(src(i * 4 * ww, 4 * ww).astype(F32))
-            return sums[0] + d1, sums[1] + d2
-
-        def dst(r0, v):
-            o_ref[s, r0:r0 + v.shape[0]] = v
-
-        sums = lax.fori_loop(0, hh // 4, in_sums, _zero_sums(n_ch))
-        blk.run(src, sums, me * n_img + s, CHUNK, dst)
+    def half_block(t, carry):
+        s, j = t // 2, lax.rem(t, 2)
+
+        @pl.when(t == 2)
+        def _():
+            _project(lambda r0, n: o_ref[0, r0:r0 + n], n_pos, (sums_ref[0, 0:1], sums_ref[0, 1:2]), grp_ref[...],
+                     anorm_v, proj_v, k_buf, q_buf, v_buf, bound_ref)
+
+        @pl.when(j == 0)
+        def _():
+            for k in range(len(peers)):
+                copy(s, k).wait_recv()
+            own(s).wait()
+
+            def take(i, sums):
+                v = xv[s, pl.ds(i * 4, 4)].reshape(4 * ww, n_ch)
+                o_ref[s, pl.ds(pl.multiple_of(i * 4 * ww, 4 * ww), 4 * ww)] = v
+                d1, d2 = _chan_sums(v.astype(F32))
+                return sums[0] + d1, sums[1] + d2
+
+            s1, s2 = lax.fori_loop(0, hh // 4, take, _zero_sums(n_ch))
+            sums_s[0:1] = s1
+            sums_s[1:2] = s2
+
+        t_row = temb_s[pl.ds(me * n_img + s, 1), :]
+
+        def epilogue(r0, acc):
+            n = acc.shape[0]
+            x = xv[s, r0 // ww:(r0 + n) // ww].reshape(n, n_ch).astype(F32)
+            out = (acc + jnp.where(j == 0, t_row, x)).astype(BF16)
+            o_ref[s, r0:r0 + n] = out
+            return out
+
+        blk.conv(j, lambda r0, n: o_ref[s, r0:r0 + n], (sums_s[0:1], sums_s[1:2]), CHUNK, epilogue)
         sums_ref[s] = sums_s[...]
         return carry
 
-    lax.fori_loop(0, n_img, image, 0)
+    lax.fori_loop(0, 2 * n_img, half_block, 0)
     for s in range(n_img):
         for k in range(len(peers)):
             copy(s, k).wait_send()
 
 
-def _last_kernel(n_row, n_col, x_ref, sums_ref, temb_ref, rnorm_ref, w_t, wtemb_ref, o_ref,
-                 yv, act, hid, temb_s, grp_s, sums_s, send_sem, recv_sem, loc_sem):
+def _last_kernel(n_row, n_col, x_ref, sums_ref, rnorm_ref, w_t, temb_ref, grp_ref, o_ref,
+                 yv, act, hid, sums_s, send_sem, recv_sem, loc_sem):
     me_r, me_c, peers = _me_and_peers(n_row, n_col)
     me = me_r * n_col + me_c
     n_img, hh, ww, n_ch = yv.shape
     bh, bw = hh // n_row, ww // n_col
-    blk = _ResBlock(hh, ww, n_ch, rnorm_ref.at[1], w_t, act, hid, temb_s, grp_s, sums_s)
-    blk.setup(temb_ref, wtemb_ref.at[1])
+    blk = _ResBlock(hh, ww, n_ch, rnorm_ref.at[1], w_t, act, hid, temb_ref, grp_ref, sums_s)
+    blk.clear_borders()
     _barrier(peers)
 
     def block(s, k, c):
@@ -299,55 +359,20 @@
         own(s).wait()
 
 
-def _attn_kernel(x_ref, sums_ref, anorm_ref, proj_ref, o_ref, osums_ref, grp_s, k_buf, q_buf, v_buf, ot_buf):
+def _attn_kernel(x_ref, sums_ref, anorm_ref, proj_ref, grp_ref, k_in, q_in, v_in, bound_in,
+                 o_ref, osums_ref, k_buf, q_buf, v_buf, bound_ref, ot_buf):
     n_img, n_pos, n_ch = x_ref.shape
-    count = float(n_pos * (n_ch // GROUPS))
-    head_dim = 32
+    head_dim, scale = HEAD_DIM, LOGIT_SCALE
     n_heads = n_ch // head_dim
     per_blk = 128 // head_dim
-    scale = LOG2E * head_dim ** -0.5
-
-    grp_s[...] = _group_matrix(n_ch)
 
     def image(img, carry_img):
-        sums = sums_ref[img, 0:1], sums_ref[img, 1:2]
-        mean, inv = _moments(*sums, grp_s[...], count)
-        a_mul = inv * anorm_ref[0:1].astype(F32)
-        b_add = anorm_ref[1:2].astype(F32)
-        head_rows = jnp.where(lax.broadcasted_iota(jnp.int32, (16, n_ch), 0)
-                              == lax.broadcasted_iota(jnp.int32, (16, n_ch), 1) // head_dim, 1.0, 0.0).astype(BF16)
-
-        q_top = jnp.zeros((n_heads, PROJ_TILE), F32)
-        k_top = jnp.zeros((16, PROJ_TILE), F32)
-        v_top = jnp.zeros((1, PROJ_TILE), F32)
-        last_k = None
-        for r0 in [*range(0, n_pos, PROJ_TILE), None]:
-            if r0 is not None:
-                tile = slice(r0, r0 + PROJ_TILE)
-                g = ((x_ref[img, tile].astype(F32) - mean) * a_mul + b_add).astype(BF16)
-                k = _dot(g, proj_ref[1], ((1,), (1,)))
-                q = _dot(proj_ref[0], g, ((1,), (1,))).astype(BF16)
-                v = _dot(proj_ref[2], g, ((1,), (1,))).astype(BF16)
-                for b0 in range(0, n_ch, 128):
-                    for j in range(per_blk):
-                        part = k[:, b0:b0 + 128]
-                        part = part if j == 0 else pltpu.roll(part, 128 - j * head_dim, 1)
-                        k_buf[j, tile, b0:b0 + 128] = part.astype(BF16)
-                k = k.astype(BF16)
-                q_buf[:, tile] = q
-                v_buf[:, tile] = v
-                q = q.astype(F32)
-                q_top = jnp.maximum(q_top, jnp.sum((q * q).reshape(n_heads, head_dim, PROJ_TILE), axis=1))
-                v_top = jnp.maximum(v_top, jnp.max(jnp.abs(v.astype(F32)), axis=0, keepdims=True))
-            if last_k is not None:
-                k2 = last_k.astype(F32) * last_k.astype(F32)
-                k_top = jnp.maximum(k_top, _dot(head_rows, k2.astype(BF16), ((1,), (1,))))
-            last_k = k
-
-        q_top = jnp.max(q_top, axis=1, keepdims=True)
-        k_top = jnp.max(k_top, axis=1, keepdims=True)[:n_heads]
-        top2 = jnp.max(q_top * k_top) * (scale * scale)
-        v_max = jnp.max(v_top)
+        @pl.when(img > 0)
+        def _():
+            _project(lambda r0, n: x_ref[img, r0:r0 + n], n_pos, (sums_ref[img, 0:1], sums_ref[img, 1:2]),
+                     grp_ref[...], anorm_ref, proj_ref, k_buf, q_buf, v_buf, bound_ref)
+
+        top2, v_max = jnp.max(bound_ref[0:1]), jnp.max(bound_ref[1:2])
         small = ((top2 < 96.0 ** 2) & (v_max < 2.0 ** 20)) | ((top2 < 108.0 ** 2) & (v_max < 2.0 ** 8))
 
         @pl.when(small)
@@ -416,7 +441,7 @@
     lax.fori_loop(0, n_img, image, 0)
 
 
-VMEM_LIMIT = 60 * 1024 * 1024
+K1_LIMIT, K2_LIMIT, K3_LIMIT = 36, 16, 24
 
 
 def solution(mesh):
@@ -430,57 +455,48 @@
         n_pos, n_img = hh * ww, n_batch // n_dev
         proj = jnp.transpose(attn_proj, (0, 1, 3, 2)).reshape(4, n_ch, n_ch)
         conv_w = res_conv.reshape(2, 2, 9 * n_ch, n_ch)
-        sums_shape = jax.ShapeDtypeStruct((n_img, 8, n_ch), F32)
         images = pltpu.VMEM((n_img, hh, ww, n_ch), BF16)
-        work = [
-            pltpu.VMEM(((hh + 2) * ww, 3 * n_ch), BF16),
-            pltpu.VMEM((n_pos, n_ch), BF16),
-            pltpu.VMEM((n_batch, n_ch), F32),
-            pltpu.VMEM((n_ch, n_ch), BF16),
-            pltpu.VMEM((8, n_ch), F32),
-        ]
+        act = pltpu.VMEM(((hh + 2) * ww, 3 * n_ch), BF16)
+        chan_sums = pltpu.VMEM((8, n_ch), F32)
         remote = [pltpu.SemaphoreType.DMA((n_img, n_dev)), pltpu.SemaphoreType.DMA((n_img, n_dev)),
                   pltpu.SemaphoreType.DMA((n_img,))]
-
-        def resident(shape, dtype=BF16):
-            return pltpu.VMEM(shape, dtype)
-
-        x1, sums1, next_w = pl.pallas_call(
+        x_out, sums_out = pltpu.VMEM((n_img, n_pos, n_ch), BF16), pltpu.VMEM((n_img, 8, n_ch), F32)
+        qkv_out = [pltpu.VMEM((128 // HEAD_DIM, n_pos, n_ch), BF16), pltpu.VMEM((n_ch, n_pos), BF16),
+                   pltpu.VMEM((n_ch, n_pos), BF16), pltpu.VMEM((8, 128), F32)]
+
+        from_hbm = (latent, t_emb, res_norm, conv_w, res_temb, attn_norm, proj)
+        x1, sums1, next_w, next_temb, grp, *qkv = pl.pallas_call(
             functools.partial(_first_kernel, n_row, n_col),
-            out_shape=[resident((n_img, n_pos, n_ch)), resident((n_img, 8, n_ch), F32), resident((2, n_ch, 9 * n_ch))],
-            in_specs=[hbm] * 5,
-            out_specs=[vmem, vmem, vmem],
+            out_shape=[x_out, sums_out, pltpu.VMEM((2, n_ch, 9 * n_ch), BF16), pltpu.VMEM((n_batch, n_ch), F32),
+                       pltpu.VMEM((n_ch, n_ch), BF16), *qkv_out],
+            in_specs=[hbm] * len(from_hbm),
+            out_specs=[vmem] * 9,
             scratch_shapes=[
                 images, pltpu.VMEM((4, 9 * n_ch, n_ch), BF16), pltpu.VMEM((2, n_ch, 9 * n_ch), BF16),
-                pltpu.VMEM(t_emb.shape, BF16), pltpu.VMEM(res_norm.shape, BF16), pltpu.VMEM(res_temb.shape[1:], BF16),
-                *work, pltpu.SemaphoreType.DMA((7,)), *remote,
+                *(pltpu.VMEM(a.shape, BF16) for a in (t_emb, res_norm, res_temb, attn_norm, proj)),
+                act, pltpu.VMEM((n_batch, n_ch), F32), chan_sums, pltpu.SemaphoreType.DMA((9,)), *remote,
             ],
-            compiler_params=pltpu.CompilerParams(collective_id=0, has_side_effects=True, vmem_limit_bytes=42 << 20),
-        )(*(pltpu.with_memory_space_constraint(a, pltpu.HBM) for a in (latent, t_emb, res_norm, conv_w, res_temb)))
-
-        x2, sums2 = pl.pallas_call(
+            compiler_params=pltpu.CompilerParams(collective_id=0, has_side_effects=True, vmem_limit_bytes=K1_LIMIT << 20),
+        )(*(pltpu.with_memory_space_constraint(a, pltpu.HBM) for a in from_hbm))
+
+        x2, sums2, *_ = pl.pallas_call(
             _attn_kernel,
-            out_shape=[resident((n_img, n_pos, n_ch)), resident((n_img, 8, n_ch), F32)],
-            in_specs=[vmem, vmem, vmem, vmem],
-            out_specs=[vmem, vmem],
-            scratch_shapes=[
-                pltpu.VMEM((n_ch, n_ch), BF16),
-                pltpu.VMEM((4, n_pos, n_ch), BF16),
-                pltpu.VMEM((n_ch, n_pos), BF16),
-                pltpu.VMEM((n_ch, n_pos), BF16),
-                pltpu.VMEM((n_ch, n_pos), BF16),
-            ],
-            compiler_params=pltpu.CompilerParams(vmem_limit_bytes=24 << 20),
-        )(x1, sums1, attn_norm, proj)
+            out_shape=[x_out, sums_out, *qkv_out],
+            in_specs=[vmem] * 9,
+            out_specs=[vmem] * 6,
+            input_output_aliases={5: 2, 6: 3, 7: 4, 8: 5},
+            scratch_shapes=[pltpu.VMEM((n_ch, n_pos), BF16)],
+            compiler_params=pltpu.CompilerParams(vmem_limit_bytes=K2_LIMIT << 20),
+        )(x1, sums1, attn_norm, proj, grp, *qkv)
 
         return pl.pallas_call(
             functools.partial(_last_kernel, n_row, n_col),
-            out_shape=resident(latent.shape),
+            out_shape=pltpu.VMEM(latent.shape, BF16),
             in_specs=[vmem] * 6,
             out_specs=vmem,
-            scratch_shapes=[images, *work, *remote],
-            compiler_params=pltpu.CompilerParams(collective_id=1, has_side_effects=True, vmem_limit_bytes=24 << 20),
-        )(x2, sums2, t_emb, res_norm, next_w, res_temb)
+            scratch_shapes=[images, act, pltpu.VMEM((n_pos, n_ch), BF16), chan_sums, *remote],
+            compiler_params=pltpu.CompilerParams(collective_id=1, has_side_effects=True, vmem_limit_bytes=K3_LIMIT << 20),
+        )(x2, sums2, res_norm, next_w, next_temb, grp)
 
     spec_x = P('dp', 'row', 'col', None)
     return jax.shard_map(run_stage, mesh=mesh, in_specs=(spec_x, P('dp', None), P(), P(), P(), P(), P()), out_specs=spec_x, check_vma=False)

time: 173 us -> 172 us (level)
  Pallas kernels: 172 us -> 170 us
    pallas_call x2, Pallas kernels: 131 us -> 128 us  [the longest x1 82.8 us: run_stage(): pl.pallas_call(functools.partial(_last_kernel, n_row, n_col), out_shape=p...]
    pallas_call x1, Pallas kernels: 41 us -> 42.9 us  [run_stage(): pl.pallas_call(functools.partial(_first_kernel, n_row, n_col), out_shape=...]
where the time goes in v3:
time: 172 us
  Pallas kernels  170 us (99%)
    pallas_call x1, Pallas kernels, run_stage(): pl.pallas_call(functools.partial(_last_kernel, n_row, n_col), out_shape=p...  82.8 us
    pallas_call x1, Pallas kernels, run_stage(): pl.pallas_call(_attn_kernel, out_shape=[x_out, sums_out, *qkv_out], in_sp...  44.7 us
    pallas_call x1, Pallas kernels, run_stage(): pl.pallas_call(functools.partial(_first_kernel, n_row, n_col), out_shape=...  42.9 us

profile of v3, /device:TPU:1, one launch (start us, length us, event | category | flops | bytes accessed | tf_op | source)
XLA Modules:
  0.0 171.9 jit_solution(12242731895787326059)
XLA Ops:
  0.0 0.0 copy-start
  0.0 0.0 copy-start.2
  0.0 42.9 %shard_map.73 = (bf16[2,1536,384]{2,1,0:T(8,128)(2,1)S(1)}, f32[2,8,384]{2,1,0:T(8,128)S(1)}, bf16[2,384,3456]{2,1,0:T(8,128)(2,1)S(1)}, f32[16,384]{1,0:T(8,128...) custom-call(bf16[16,4,48,384]{3,2,1,0:T(8,128)(2,1)} %lat_ref.1, ...), custom_call_target="tpu_custom_call" | custom-call | tf_op jit(solution)/shard_map/pallas_call | solution.py:468
  42.9 0.0 copy-done
  42.9 0.0 copy-done.2
  42.9 0.0 copy-start.1
  42.9 44.7 %shard_map.74 = (bf16[2,1536,384]{2,1,0:T(8,128)(2,1)S(1)}, f32[2,8,384]{2,1,0:T(8,128)S(1)}, bf16[4,1536,384]{2,1,0:T(8,128)(2,1)S(1)}, bf16[384,1536]{1,0:T(8,...) custom-call(bf16[2,1536,384]{2,1,0:T(8,128)(2,1)S(1)} %get-tuple-ele, ...), custom_call_target="tpu_custom_call", output_to_operand_aliasing={{2}: (5, {}), {3}: (6, {}), {4}: (7, {}), {5}: (8, {})} | custom-call | tf_op jit(solution)/shard_map/pallas_call | solution.py:482
  87.7 0.0 copy-done.1
  87.7 82.8 %shard_map.75 = bf16[16,4,48,384]{3,2,1,0:T(8,128)(2,1)S(1)} custom-call(bf16[2,1536,384]{2,1,0:T(8,128)(2,1)S(1)} %get-tuple-element.23.x_ref, f32[2,8,384]{2,1,0:T(8,128)S(1)} %get-tuple-element.24.sums_ref, bf16[2,2,2,384]{3,2,1,0:T(2,128)(2,1)S(1)} %copy-done.1, bf16[2,384,3456]{2,1,0:T(8,128)(2,1)S(1)} %get-tuple-element.25.w_t, ...), custom_call_target="tpu_custom_call" | custom-call | tf_op jit(solution)/shard_map/pallas_call | solution.py:492
  170.5 1.4 copy.17
Async XLA Ops:
  0.0 42.9 %copy-start = (bf16[4,12,384,32]{2,3,1,0:T(8,128)(2,1)S(1)}, bf16[4,12,384,32]{2,3,1,0:T(8,128)(2,1)}, u32[]{:S(2)}) copy-start(bf16[4,12,384,32]{2,3,1,0:T(8,128)(2,1)} %param.13) | copy-start | bytes 3538948
  0.0 42.9 %copy-start.2 = (bf16[2,384]{1,0:T(2,128)(2,1)S(1)}, bf16[2,384]{1,0:T(2,128)(2,1)}, u32[]{:S(2)}) copy-start(bf16[2,384]{1,0:T(2,128)(2,1)} %anorm_ref.1) | copy-start | bytes 4612
  42.9 44.8 %copy-start.1 = (bf16[2,2,2,384]{3,2,1,0:T(2,128)(2,1)S(1)}, bf16[2,2,2,384]{3,2,1,0:T(2,128)(2,1)}, u32[]{:S(2)}) copy-start(bf16[2,2,2,384]{3,2,1,0:T(2,128)(2,1)} %rnorm_ref.1) | copy-start | bytes 18436
